TPU v7x, 32 devices: a whole 2x2x4 slice. The times are simulated.
32 devices in a mesh: tm: 32 (over z, y, x, core), prod: 1.
Axes of the slice: x: 2, y: 2, z: 4, core: 2. Of those that a mesh axis runs over, the one named last changes fastest.
Arguments:
- sales_records: float32 [1024, 16, 16, 128], P('tm', 'prod'), may hold values from -6 to 6
- day_month: int32 [1024], replicated, may hold values from 0 to 31, as said below
- month_year: int32 [32], replicated, may hold values from 0 to 3, never falling along the last dimension, each value on 1 to 16 neighbouring positions
- product_category: int32 [16], replicated, may hold values from 0 to 31
- store_region: int32 [16], replicated, may hold values from 0 to 3
Outputs:
- month_detail: float32 [32, 32, 4, 128], P('tm', 'prod')
- month_category: float32 [32, 32, 128], P('tm', 'prod')
- month_region: float32 [32, 4, 128], P('tm')
- month_totals: float32 [32, 128], P('tm')
- year_detail: float32 [4, 32, 4, 128], replicated
- year_category: float32 [4, 32, 128], replicated
- year_region: float32 [4, 4, 128], replicated
- year_totals: float32 [4, 128], replicated
Inputs may be any that keep to these rules, and one draw needn't show every extreme that they name: `day_month`: never falls along the days; month m, for m of 1 to 31, begins at a day from m * 32 - 31 // 2 to m * 32 + 31 // 2, and both ends of that range are taken in every draw. `month_year`: never falls along the months; every year has 1 to 16 months, one exactly that many.
All inputs are finite; a program needn't handle non-finite values.
Results may differ from a plain program's by a relative error of at most 0.0001.
Values sent between devices are 32-bit elements; how exact they have to be, the bound alone decides.
No kernel may reach another device: no remote copies, remote signals or barrier semaphores. Data moves between devices by JAX's collectives and lax.ppermute only.
A program may use at most 64 MiB of HBM per device.

v0:
```python
import jax
import jax.numpy as jnp
from jax import lax
from jax.sharding import PartitionSpec as P

MON_DEV = 1
CATEGORY_COUNT = 32
REGION_COUNT = 4


def with_halo(block, sides, width):
    for axis, dim in sides:
        count = lax.axis_size(axis)
        forward = [(i, i + 1) for i in range(count - 1)]
        backward = [(target, source) for source, target in forward]
        low = lax.ppermute(
            lax.slice_in_dim(block, block.shape[dim] - width, None, axis=dim), axis, forward
        )
        high = lax.ppermute(lax.slice_in_dim(block, 0, width, axis=dim), axis, backward)
        block = jnp.concatenate([low, block, high], axis=dim)
    return block


def onehot(labels, width):
    return (labels[:, None] == jnp.arange(width, dtype=jnp.int32)[None, :]).astype(jnp.float32)


def scaled(sums, counts):
    return sums / jnp.sqrt(counts)


def shards(sales_records, day_month, month_year, product_category, store_region):
    highest = lax.Precision.HIGHEST
    day_dev = sales_records.shape[0]
    prod_dev = sales_records.shape[1]
    stores = float(sales_records.shape[2])
    month_width = month_year.shape[0]
    year_width = max(month_width // 8, 2)
    cats_dev = CATEGORY_COUNT // lax.axis_size("prod")
    products = float(prod_dev * lax.axis_size("prod"))
    time_index = lax.axis_index("tm")
    prod_index = lax.axis_index("prod")
    month_hot = onehot(day_month, month_width)
    year_hot = onehot(month_year, year_width)
    category_hot = onehot(product_category, CATEGORY_COUNT)
    region_hot = onehot(store_region, REGION_COUNT)
    local_products = lax.dynamic_slice_in_dim(category_hot, prod_index * prod_dev, prod_dev, 0)
    by_region = jnp.einsum("dpsq,sr->dprq", sales_records, region_hot, precision=highest)
    by_category = jnp.einsum("dprq,pc->dcrq", by_region, local_products, precision=highest)
    month_days = jnp.sum(month_hot, 0)
    year_days = jnp.dot(month_days, year_hot, precision=highest)
    category_size = jnp.sum(category_hot, 0)
    region_size = jnp.sum(region_hot, 0)
    own_days = lax.dynamic_slice_in_dim(month_days, time_index * MON_DEV, MON_DEV, 0)
    own_sizes = lax.dynamic_slice_in_dim(category_size, prod_index * cats_dev, cats_dev, 0)
    local_labels = lax.dynamic_slice_in_dim(day_month, time_index * day_dev, day_dev, 0)
    window_ids = time_index - 1 + jnp.arange(3, dtype=jnp.int32)
    window_hot = (local_labels[:, None] == window_ids[None, :]).astype(jnp.float32)
    partial_value = jnp.einsum("dcrq,dk->kcrq", by_category, window_hot, precision=highest)
    clipped = jnp.clip(window_ids, 0, month_width - 1)
    inside = ((window_ids >= 0) & (window_ids < month_width)).astype(jnp.float32)
    source_years = onehot(month_year[clipped], year_width) * inside[:, None]
    padded = with_halo(partial_value, (("tm", 0),), 1)
    summed = padded[0:1] + padded[2:3] + padded[4:5]
    detail = lax.psum_scatter(summed, "prod", scatter_dimension=1, tiled=True)
    year_part = jnp.einsum("mcrq,my->ycrq", partial_value, source_years, precision=highest)
    year_cube = lax.psum(year_part, ("tm", "prod"))
    cell = own_days[:, None, None] * own_sizes[None, :, None] * region_size[None, None, :]
    month_detail = scaled(detail, jnp.maximum(cell, 1.0)[..., None])
    month_cat = jnp.sum(detail, 2)
    month_category = scaled(
        month_cat, jnp.maximum(own_days[:, None] * own_sizes[None, :] * stores, 1.0)[..., None]
    )
    month_reg = lax.psum(jnp.sum(detail, 1), "prod")
    month_region = scaled(
        month_reg, jnp.maximum(own_days[:, None] * products * region_size[None, :], 1.0)[..., None]
    )
    month_totals = scaled(jnp.sum(month_reg, 1), (own_days * products * stores)[:, None])
    year_cell = year_days[:, None, None] * category_size[None, :, None] * region_size[None, None, :]
    year_detail = scaled(year_cube, jnp.maximum(year_cell, 1.0)[..., None])
    year_cat = jnp.sum(year_cube, 2)
    year_category = scaled(
        year_cat, jnp.maximum(year_days[:, None] * category_size[None, :] * stores, 1.0)[..., None]
    )
    year_reg = jnp.sum(year_cube, 1)
    year_region = scaled(
        year_reg, jnp.maximum(year_days[:, None] * products * region_size[None, :], 1.0)[..., None]
    )
    year_totals = scaled(jnp.sum(year_reg, 1), (year_days * products * stores)[:, None])
    return (
        month_detail,
        month_category,
        month_region,
        month_totals,
        year_detail,
        year_category,
        year_region,
        year_totals,
    )


def solution(mesh):
    placed = (P("tm", "prod", None, None), P(), P(), P(), P())
    return jax.shard_map(
        shards,
        mesh=mesh,
        in_specs=placed,
        out_specs=(
            P("tm", "prod", None, None),
            P("tm", "prod", None),
            P("tm", None, None),
            P("tm", None),
            P(),
            P(),
            P(),
            P(),
        ),
        check_vma=False,
    )
```

profile of v0, /device:TPU:0, one launch (start us, length us, event | category | flops | bytes accessed | tf_op | source)
XLA Modules:
  0.0 163.1 jit_solution(17972851459997069887)
XLA Ops:
  7.2 3.8 %convolution_bitcast_fusion.1 = f32[32,16,4,128]{3,2,1,0:T(4,128)S(1)} fusion(f32[32,16,16,128]{3,2,1,0:T(8,128)} %param.5, s32[16]{0:T(128)} %param.9), kind=kOutput, calls=%fused_computation.4 | convolution fusion | flops 50331712 | bytes 5242944 | tf_op jit(solution)/shard_map/dpsq,sr->dprq/dot_general | solution.py:48
  11.0 1.1 convolution_bitcast_fusion
  12.2 0.1 dynamic_slice.8
  12.3 2.5 %fusion = f32[3,32,4,128]{3,0,2,1:T(4,128)S(1)} fusion(f32[32,32,4,128]{3,1,2,0:T(8,128)S(1)} %convolution_bitcast_fusion, s32[32]{0:T(128)S(1)} %dynamic_slice.8, s32[3]{0:T(128)S(1)} %iota_add_fusion), kind=kOutput, calls=%fused_computation.1 | convolution fusion | flops 18874464 | bytes 2293900 | tf_op jit(solution)/shard_map/dcrq,dk->kcrq/dot_general | solution.py:59
  14.7 0.1 fusion.27
  14.8 1.3 collective-permute-start.1
  16.1 3.0 %collective-permute-start = (f32[1,32,4,128]{3,0,2,1:T(1,128)S(1)}, f32[1,32,4,128]{3,0,2,1:T(1,128)S(1)}, u32[]{:S(2)}, u32[]{:S(2)}) collective-permute-start(f32[1,32,4,128]{3,0,2,1:T(1,128)S(1)} %get-tuple-element.58), channel_id=1, source_target_pairs={{0,1},{1,2},{2,3},{3,4},{4,5},{5,6},{6,7},{7,8},{8,9},{9,10},{10,1... | collective-permute-start | bytes 196616 | tf_op jit(solution)/shard_map/ppermute | solution.py:16
  19.2 0.6 gather_fusion
  19.9 1.3 fusion.8
  21.2 0.1 convert_reduce_fusion.2
  21.3 0.1 convert_reduce_fusion.1
  21.4 0.1 convert_reduce_fusion
  21.5 0.2 multiply_sqrt_fusion
  21.7 0.6 dynamic_slice.9
  22.9 0.7 maximum_sqrt_fusion.5
  23.8 0.1 maximum_sqrt_fusion
  23.8 0.1 maximum_sqrt_fusion.1
  23.9 0.1 copy.33
  24.7 0.1 copy.34
  24.8 0.1 copy.35
  24.9 0.2 fusion.25
  25.1 0.8 broadcast_divide_fusion.2
  26.0 0.7 bitcast_divide_fusion
  26.6 0.7 bitcast_divide_fusion.1
  27.3 0.5 divide_bitcast_fusion
  27.8 124.4 %all-reduce.2.cloned.1.call-done = f32[4,32,4,128]{3,0,2,1:T(4,128)} async-done(((f32[4,32,4,128]{3,0,2,1:T(4,128)}), f32[4,32,4,128]{3,0,2,1:T(4,128)}) %all-reduce.2.cloned.1.call-update) | async-done | bytes 262160 | tf_op jit(solution)/shard_map/psum | solution.py:67
  152.2 1.2 fusion.24
  153.4 0.8 copy.37
  154.1 0.1 broadcast_divide_fusion.1
  154.2 0.6 copy.38
  154.9 0.6 copy.39
  155.6 0.7 broadcast_divide_fusion.4
  (20 shorter events, 0.3 us)
Async XLA Ops:
  7.2 145.0 %all-reduce.2.cloned.1.call-start = ((), (), s32[]{:S(2)}) async-start(), calls=%async_computation | async-start | bytes 524288 | tf_op jit(solution)/shard_map/psum | solution.py:67
  7.2 3.8 %copy-start.2 = (s32[16]{0:T(128)S(1)}, s32[16]{0:T(128)}, u32[]{:S(2)}) copy-start(s32[16]{0:T(128)} %param.8) | copy-start | bytes 196
  11.0 1.2 copy-start.1
  12.1 7.1 %copy-start = (s32[32]{0:T(128)S(1)}, s32[32]{0:T(128)}, u32[]{:S(2)}) copy-start(s32[32]{0:T(128)} %param.7) | copy-start | bytes 388
  12.2 9.0 %copy-start.3 = (s32[16]{0:T(128)S(1)}, s32[16]{0:T(128)}, u32[]{:S(2)}) copy-start(s32[16]{0:T(128)} %param.9) | copy-start | bytes 196
  14.8 10.1 %collective-permute-start.1 = (f32[1,32,4,128]{3,0,2,1:T(1,128)S(1)}, f32[1,32,4,128]{3,0,2,1:T(1,128)S(1)}, u32[]{:S(2)}, u32[]{:S(2)}) collective-permute-start(f32[1,32,4,128]{3,0,2,1:T(1,128)S(1)} %get-tuple-element.59), channel_id=1, source_target_pairs={{1,0},{2,1},{3,2},{4,3},{5,4},{6,5},{7,6},{8,7},{9,8},{10,9},{11,1... | collective-permute-start | bytes 196616 | tf_op jit(solution)/shard_map/ppermute | solution.py:19
  16.1 8.8 %collective-permute-start = (f32[1,32,4,128]{3,0,2,1:T(1,128)S(1)}, f32[1,32,4,128]{3,0,2,1:T(1,128)S(1)}, u32[]{:S(2)}, u32[]{:S(2)}) collective-permute-start(f32[1,32,4,128]{3,0,2,1:T(1,128)S(1)} %get-tuple-element.58), channel_id=1, source_target_pairs={{0,1},{1,2},{2,3},{3,4},{4,5},{5,6},{6,7},{7,8},{8,9},{9,10},{10,1... | collective-permute-start | bytes 196616 | tf_op jit(solution)/shard_map/ppermute | solution.py:16
Sparse Core Ops, SparseCore 0:
  21.3 130.8 all-reduce.1
where the time goes:
time: 163 us
  waiting for transfers between devices  124 us (76%)
  between operations  15.6 us (10%)
  matrix products  8.79 us (5%)
  other arithmetic  6.2 us (4%)
  starting transfers between devices  4.36 us (3%)
  local copies, waits for them, and re-layouts  3.75 us (2%)
    psum x1, waiting for transfers between devices, shards(): year_cube = lax.psum(year_part, ('tm', 'prod'))  124 us
    dot_general x1, matrix products, shards(): jnp.einsum('dpsq,sr->dprq', sales_records, region_hot, precision=highest)  3.76 us
    div x7, other arithmetic, scaled(): return sums / jnp.sqrt(counts)  3.52 us
  transfers between devices with their start and end apart: 3, of which 1 were waited for; matrix products, arithmetic and copies ran while one was open for 4% of the time, Pallas kernels for 0%

commit v1 on v0

--- a/solution.py
+++ b/solution.py
@@ -64,7 +64,7 @@
     summed = padded[0:1] + padded[2:3] + padded[4:5]
     detail = lax.psum_scatter(summed, "prod", scatter_dimension=1, tiled=True)
     year_part = jnp.einsum("mcrq,my->ycrq", partial_value, source_years, precision=highest)
-    year_cube = lax.psum(year_part, ("tm", "prod"))
+    year_cube = jnp.sum(lax.all_gather(year_part, ("tm", "prod")), axis=0)
     cell = own_days[:, None, None] * own_sizes[None, :, None] * region_size[None, None, :]
     month_detail = scaled(detail, jnp.maximum(cell, 1.0)[..., None])
     month_cat = jnp.sum(detail, 2)

time: 163 us -> 117 us (0.72)
  waiting for transfers between devices: 124 us -> 69.5 us
  other arithmetic: 6.2 us -> 14.8 us
    psum x1 -> x0, waiting for transfers between devices: 124 us -> none  [shards(): year_cube = lax.psum(year_part, ('tm', 'prod'))]
    all_gather x0 -> x1, waiting for transfers between devices: none -> 69.3 us  [shards(): year_cube = jnp.sum(lax.all_gather(year_part, ('tm', 'prod')), axis=0)]
    reduce_sum x0 -> x1, other arithmetic: none -> 4.26 us  [shards(): year_cube = jnp.sum(lax.all_gather(year_part, ('tm', 'prod')), axis=0)]
    reduce_sum x1 -> x2, other arithmetic: 1.18 us -> 5.04 us  [shards(): jnp.sum(year_reg, 1)]
    div x7 -> x8, other arithmetic: 3.52 us -> 3.77 us  [scaled(): return sums / jnp.sqrt(counts)]
  transfers between devices with their start and end apart: 3 -> 3, of which waited for: 1 -> 2; matrix products, arithmetic and copies ran while one was open for 4% -> 5% of each run, Pallas kernels for 0% -> 0%
where the time goes in v1:
time: 117 us
  waiting for transfers between devices  69.5 us (59%)
  between operations  15.6 us (13%)
  other arithmetic  14.8 us (13%)
  matrix products  8.1 us (7%)
  local copies, waits for them, and re-layouts  5.2 us (4%)
  starting transfers between devices  3.73 us (3%)
    all_gather x1, waiting for transfers between devices, shards(): year_cube = jnp.sum(lax.all_gather(year_part, ('tm', 'prod')), axis=0)  69.3 us
    reduce_sum x2, other arithmetic, shards(): jnp.sum(year_reg, 1)  5.04 us
    reduce_sum x1, other arithmetic, shards(): year_cube = jnp.sum(lax.all_gather(year_part, ('tm', 'prod')), axis=0)  4.26 us
    div x8, other arithmetic, scaled(): return sums / jnp.sqrt(counts)  3.77 us
    dot_general x1, matrix products, shards(): jnp.einsum('dpsq,sr->dprq', sales_records, region_hot, precision=highest)  3.76 us
    dot_general x1, matrix products, shards(): jnp.einsum('dcrq,dk->kcrq', by_category, window_hot, precision=highest)  2.46 us
    ppermute x1, starting transfers between devices, with_halo(): lax.ppermute(lax.slice_in_dim(block, block.shape[dim] - width, None, axis...  2.4 us
  transfers between devices with their start and end apart: 3, of which 2 were waited for; matrix products, arithmetic and copies ran while one was open for 5% of the time, Pallas kernels for 0%

profile of v1, /device:TPU:0, one launch (start us, length us, event | category | flops | bytes accessed | tf_op | source)
XLA Modules:
  0.0 116.8 jit_solution(17558224526090363138)
XLA Ops:
  7.3 0.8 dynamic_slice.8
  8.0 3.8 %convolution_bitcast_fusion.1 = f32[32,16,4,128]{3,2,1,0:T(4,128)S(1)} fusion(f32[32,16,16,128]{3,2,1,0:T(8,128)} %param.5, s32[16]{0:T(128)} %param.9), kind=kOutput, calls=%fused_computation.4 | convolution fusion | flops 50331712 | bytes 5242944 | tf_op jit(solution)/shard_map/dpsq,sr->dprq/dot_general | solution.py:48
  11.8 1.1 convolution_bitcast_fusion
  13.0 0.6 gather_fusion
  13.6 2.5 %fusion = f32[3,32,4,128]{3,0,2,1:T(4,128)S(1)} fusion(f32[32,32,4,128]{3,1,2,0:T(8,128)S(1)} %convolution_bitcast_fusion, s32[32]{0:T(128)S(1)} %dynamic_slice.8, s32[3]{0:T(128)S(1)} %iota_add_fusion), kind=kOutput, calls=%fused_computation.1 | convolution fusion | flops 18874464 | bytes 2293900 | tf_op jit(solution)/shard_map/dcrq,dk->kcrq/dot_general | solution.py:59
  16.1 0.6 fusion.8
  16.6 0.8 copy.58
  17.4 0.1 fusion.27
  17.6 2.4 %collective-permute-start = (f32[1,32,4,128]{3,0,2,1:T(1,128)S(1)}, f32[1,32,4,128]{3,0,2,1:T(1,128)S(1)}, u32[]{:S(2)}, u32[]{:S(2)}) collective-permute-start(f32[1,32,4,128]{3,0,2,1:T(1,128)S(1)} %get-tuple-element.73), channel_id=1, source_target_pairs={{0,1},{1,2},{2,3},{3,4},{4,5},{5,6},{6,7},{7,8},{8,9},{9,10},{10,1... | collective-permute-start | bytes 196616 | tf_op jit(solution)/shard_map/ppermute | solution.py:16
  20.0 1.3 %collective-permute-start.1 = (f32[1,32,4,128]{3,0,2,1:T(1,128)S(1)}, f32[1,32,4,128]{3,0,2,1:T(1,128)S(1)}, u32[]{:S(2)}, u32[]{:S(2)}) collective-permute-start(f32[1,32,4,128]{3,0,2,1:T(1,128)S(1)} %get-tuple-element.74), channel_id=1, source_target_pairs={{1,0},{2,1},{3,2},{4,3},{5,4},{6,5},{7,6},{8,7},{9,8},{10,9},{11,1... | collective-permute-start | bytes 196616 | tf_op jit(solution)/shard_map/ppermute | solution.py:19
  21.3 0.1 convert_reduce_fusion
  21.4 0.6 dynamic_slice.9
  22.7 0.1 convert_reduce_fusion.2
  22.9 0.7 maximum_sqrt_fusion.5
  23.5 0.2 multiply_sqrt_fusion
  24.8 0.1 copy.60
  25.0 0.2 collective-permute-done.1
  25.2 0.2 fusion.25
  25.4 0.5 divide_bitcast_fusion
  25.9 0.7 bitcast_divide_fusion.1
  26.6 0.7 bitcast_divide_fusion
  27.2 0.8 broadcast_divide_fusion
  28.1 69.3 %all-gather.3.cloned.1.call-done = f32[128,32,4,128]{3,1,2,0:T(8,128)} async-done(((f32[4,32,4,128]{3,1,2,0:T(8,128)}), f32[128,32,4,128]{3,1,2,0:T(8,128)}) %all-gather.3.cloned.1.call-update) | async-done | bytes 8388624 | tf_op jit(solution)/shard_map/all_gather | solution.py:67
  97.4 5.0 %fusion.24 = (f32[128,128]{1,0:T(8,128)S(1)}, f32[128,32,128]{2,1,0:T(8,128)S(1)}, f32[128,4,128]{2,1,0:T(4,128)S(1)}) fusion(f32[128,32,4,128]{3,1,2,0:T(8,128)} %all-gather.3.cloned.1.call-done), kind=kLoop, calls=%fused_computation.57 | loop fusion | flops 5685248 | bytes 10813440 | tf_op jit(solution)/shard_map/reduce_sum | solution.py:89
  102.5 0.6 copy.68
  103.1 4.3 %reduce_sum.102 = f32[4,32,4,128]{3,1,2,0:T(8,128)S(1)} reduce(f32[32,4,32,4,128]{4,2,3,1,0:T(8,128)} %bitcast.53, f32[]{:T(128)} %constant.17.clone.1), dimensions={0}, to_apply=%region_6.7 | reduce | flops 2031616 | bytes 8650756 | tf_op jit(solution)/shard_map/reduce_sum | solution.py:67
  107.4 0.2 copy_divide_fusion
  107.6 0.8 copy.66
  108.4 0.1 reduce.14
  108.6 0.1 copy_divide_fusion.1
  108.7 0.6 copy.67
  109.3 0.7 broadcast_divide_fusion.1
  (26 shorter events, 0.9 us)
Async XLA Ops:
  7.2 90.2 %all-gather.3.cloned.1.call-start = ((), (), s32[]{:S(2)}) async-start(), calls=%async_computation | async-start | bytes 8650752 | tf_op jit(solution)/shard_map/all_gather | solution.py:67
  8.0 3.8 %copy-start.2 = (s32[16]{0:T(128)S(1)}, s32[16]{0:T(128)}, u32[]{:S(2)}) copy-start(s32[16]{0:T(128)} %param.8) | copy-start | bytes 196
  11.8 1.1 copy-start
  13.6 7.7 %copy-start.1 = (s32[1024]{0:T(1024)S(1)}, s32[1024]{0:T(1024)}, u32[]{:S(2)}) copy-start(s32[1024]{0:T(1024)} %param.6) | copy-start | bytes 12292
  13.6 9.0 %copy-start.3 = (s32[16]{0:T(128)S(1)}, s32[16]{0:T(128)}, u32[]{:S(2)}) copy-start(s32[16]{0:T(128)} %param.9) | copy-start | bytes 196
  17.6 7.5 %collective-permute-start = (f32[1,32,4,128]{3,0,2,1:T(1,128)S(1)}, f32[1,32,4,128]{3,0,2,1:T(1,128)S(1)}, u32[]{:S(2)}, u32[]{:S(2)}) collective-permute-start(f32[1,32,4,128]{3,0,2,1:T(1,128)S(1)} %get-tuple-element.73), channel_id=1, source_target_pairs={{0,1},{1,2},{2,3},{3,4},{4,5},{5,6},{6,7},{7,8},{8,9},{9,10},{10,1... | collective-permute-start | bytes 196616 | tf_op jit(solution)/shard_map/ppermute | solution.py:16
  20.0 5.2 %collective-permute-start.1 = (f32[1,32,4,128]{3,0,2,1:T(1,128)S(1)}, f32[1,32,4,128]{3,0,2,1:T(1,128)S(1)}, u32[]{:S(2)}, u32[]{:S(2)}) collective-permute-start(f32[1,32,4,128]{3,0,2,1:T(1,128)S(1)} %get-tuple-element.74), channel_id=1, source_target_pairs={{1,0},{2,1},{3,2},{4,3},{5,4},{6,5},{7,6},{8,7},{9,8},{10,9},{11,1... | collective-permute-start | bytes 196616 | tf_op jit(solution)/shard_map/ppermute | solution.py:19
Sparse Core Ops, SparseCore 0:
  17.6 79.7 all-gather.2
